TPU v7x, 32 devices: a whole 2x2x4 slice. The times are simulated.
32 devices in a mesh: dp: 4 (over z), task: 4 (over y, x), mp: 2 (over core).
Axes of the slice: x: 2, y: 2, z: 4, core: 2. Of those that a mesh axis runs over, the one named last changes fastest.
Arguments:
- deltas: bfloat16 [4, 2, 128, 28672], P('task', None, 'dp', 'mp'), may hold values from -3.984375 to 3.984375, as said below
- keep_blocks: int32 [4, 2, 1], P('task'), may hold values 0 or 1
- base_weights: bfloat16 [2, 128, 28672], P(None, 'dp', 'mp'), may hold values from -6 to 6
Outputs:
- merged: float32 [2, 128, 28672], P(None, 'dp', 'mp')
Inputs may be any that keep to these rules, and one draw needn't show every extreme that they name: `deltas`: every entry is a whole multiple of 1/64.
All inputs are finite; a program needn't handle non-finite values. No bound on the sum of `keep_blocks` on one device may be relied on, other than what follows from the above.
Results may differ from a plain program's by a relative error of at most 0.0003.
Values may be sent and summed in bfloat16 or wider, within the bound.
No kernel may reach another device: no remote copies, remote signals or barrier semaphores. Data moves between devices by JAX's collectives and lax.ppermute only.
A program may use at most 128 MiB of HBM per device.

v0:
```python
import jax
import jax.numpy as jnp
from jax import lax
from jax.sharding import PartitionSpec as P

BLOCK = 128


def combine(totals, own_base):
    upward, downward, up_count, down_count = totals
    elected = jnp.sign(upward + downward)
    upper_mean = upward / jnp.maximum(up_count, 1.0)
    lower_mean = downward / jnp.maximum(down_count, 1.0)
    agreed = jnp.where(elected > 0, upper_mean, jnp.where(elected < 0, lower_mean, 0.0))
    return own_base.astype(jnp.float32) + agreed


def statistics(trimmed):
    upward = jnp.maximum(trimmed, 0.0)
    downward = jnp.minimum(trimmed, 0.0)
    up_count = (trimmed > 0).astype(jnp.float32)
    down_count = (trimmed < 0).astype(jnp.float32)
    return (upward, downward, up_count, down_count)


def on_device(deltas, keep_blocks, base_weights):
    row_count = deltas.shape[2]
    block_count = keep_blocks.shape[2]
    row_start = lax.axis_index("dp") * row_count
    block_of_row = (row_start + jnp.arange(row_count, dtype=jnp.int32)) // BLOCK
    block_hits = (
        block_of_row[:, None] == jnp.arange(block_count, dtype=jnp.int32)[None, :]
    ).astype(jnp.float32)
    row_keep = jnp.dot(keep_blocks[0].astype(jnp.float32), block_hits.T)
    trimmed = deltas[0].astype(jnp.float32) * row_keep[:, :, None]
    share_rows = row_count // lax.axis_size("task")
    sendable = trimmed.astype(jnp.bfloat16)[None]
    arrived = lax.all_to_all(sendable, "task", split_axis=2, concat_axis=0, tiled=True)
    upward, downward, up_count, down_count = statistics(arrived.astype(jnp.float32))
    totals = (
        jnp.sum(upward, axis=0),
        jnp.sum(downward, axis=0),
        jnp.sum(up_count, axis=0),
        jnp.sum(down_count, axis=0),
    )
    own_base = lax.dynamic_slice_in_dim(
        base_weights, lax.axis_index("task") * share_rows, share_rows, 1
    )
    merged_part = combine(totals, own_base)
    return lax.all_gather(merged_part, "task", axis=1, tiled=True)


def solution(mesh):
    in_specs = (P("task", None, "dp", "mp"), P("task", None, None), P(None, "dp", "mp"))
    out_specs = P(None, "dp", "mp")
    return jax.shard_map(
        on_device, mesh=mesh, in_specs=in_specs, out_specs=out_specs, check_vma=False
    )
```

profile of v0, /device:TPU:0, one launch (start us, length us, event | category | flops | bytes accessed | tf_op | source)
XLA Modules:
  0.0 144.1 jit_solution(11220083097380174780)
XLA Ops:
  6.5 0.0 copy-start
  6.5 0.8 convert_bitcast_fusion
  7.3 0.1 multiply_bitcast_fusion
  7.4 1.9 %multiply_convert_fusion = bf16[1,2,32,14336]{3,2,1,0:T(8,128)(2,1)S(1)} fusion(bf16[1,2,32,14336]{3,2,1,0:T(8,128)(2,1)} %param.3, f32[2,32]{1,0:T(2,128)S(1)} %multiply_bitcast_fusion), kind=kLoop, calls=%fused_computation.4 | loop fusion | flops 2752512 | bytes 3670272 | tf_op jit(solution)/shard_map/convert_element_type | solution.py:37
  9.3 3.1 %copy.12 = bf16[1,2,32,14336]{3,1,0,2:T(2,128)(2,1)} copy(bf16[1,2,32,14336]{3,2,1,0:T(8,128)(2,1)S(1)} %multiply_convert_fusion) | data formatting | bytes 3670016 | tf_op jit(solution)/shard_map/convert_element_type | solution.py:37
  12.4 5.2 %all-to-all-start = ((bf16[1,2,32,14336]{3,1,0,2:T(2,128)(2,1)}), bf16[1,2,32,14336]{3,1,0,2:T(2,128)(2,1)}, u32[]{:S(2)}, u32[]{:S(2)}) async-start(bf16[1,2,32,14336]{3,1,0,2:T(2,128)(2,1)} %copy.12), calls=%async_computation | async-start | bytes 3670016 | tf_op jit(solution)/shard_map/all_to_all | solution.py:38
  17.6 0.0 all-gather.2.cloned.1.call-start
  17.6 0.0 copy-done
  17.7 22.8 %all-to-all-done = bf16[1,2,32,14336]{3,1,0,2:T(2,128)(2,1)} async-done(((bf16[1,2,32,14336]{3,1,0,2:T(2,128)(2,1)}), bf16[1,2,32,14336]{3,1,0,2:T(2,128)(2,1)}, u32[]{:S(2)}, u32[]{:S(2)}) %all-to-all-start) | async-done | bytes 1835040 | tf_op jit(solution)/shard_map/all_to_all | solution.py:38
  40.5 8.5 %compare_convert_fusion.1 = (f32[1,2,32,14336]{3,1,0,2:T(2,128)}, f32[1,2,32,14336]{3,1,0,2:T(2,128)}) fusion(bf16[1,2,32,14336]{3,1,0,2:T(2,128)(2,1)} %all-to-all-done), kind=kLoop, calls=%fused_computation.1 | loop fusion | flops 4587520 | bytes 9175040 | tf_op jit(solution)/shard_map/convert_element_type | solution.py:21
  49.0 4.3 %reduce.10 = f32[2,8,14336]{2,0,1:T(2,128)S(1)} reduce(f32[2,4,8,14336]{3,0,2,1:T(2,128)} %bitcast.11, f32[]{:T(128)} %constant.35.clone.1), dimensions={1}, to_apply=%region_2.3 | reduce | flops 688128 | bytes 4587524 | tf_op jit(solution)/shard_map/reduce_sum | solution.py:43
  53.3 5.3 %reduce.11 = f32[2,8,14336]{2,0,1:T(2,128)} reduce(f32[2,4,8,14336]{3,0,2,1:T(2,128)} %bitcast.9, f32[]{:T(128)} %constant.35.clone.1), dimensions={1}, to_apply=%region_3.4 | reduce | flops 688128 | bytes 4587524 | tf_op jit(solution)/shard_map/reduce_sum | solution.py:44
  58.6 8.5 %convert_maximum_fusion = (f32[1,2,32,14336]{3,1,0,2:T(2,128)}, f32[1,2,32,14336]{3,1,0,2:T(2,128)}) fusion(bf16[1,2,32,14336]{3,1,0,2:T(2,128)(2,1)} %all-to-all-done), kind=kLoop, calls=%fused_computation.3 | loop fusion | flops 2752512 | bytes 9175040 | tf_op jit(solution)/shard_map/max | solution.py:19
  67.1 5.5 %reduce_sum.36 = f32[2,8,14336]{2,0,1:T(2,128)} reduce(f32[2,4,8,14336]{3,0,2,1:T(2,128)} %bitcast.10, f32[]{:T(128)} %constant.35.clone.1), dimensions={1}, to_apply=%region_0.1 | reduce | flops 688128 | bytes 4587524 | tf_op jit(solution)/shard_map/reduce_sum | solution.py:41
  72.5 5.3 %reduce_sum.37 = f32[2,8,14336]{2,0,1:T(2,128)} reduce(f32[2,4,8,14336]{3,0,2,1:T(2,128)} %bitcast.8, f32[]{:T(128)} %constant.35.clone.1), dimensions={1}, to_apply=%region_1.2 | reduce | flops 688128 | bytes 4587524 | tf_op jit(solution)/shard_map/reduce_sum | solution.py:42
  77.8 4.6 %convert_add_fusion = f32[2,8,14336]{2,0,1:T(2,128)} fusion(f32[2,8,14336]{2,0,1:T(2,128)} %reduce_sum.37, f32[2,8,14336]{2,0,1:T(2,128)} %reduce.11, f32[2,8,14336]{2,0,1:T(2,128)} %reduce_sum.36, f32[2,8,14336]{2,0,1:T(2,128)S(1)} %reduce.10, bf16[2,8,14336]{2,1,0:T(8,128)(2,1)S(1)} %constant_dynamic-slice_fusion), kind=kLoop, calls=%fused_computation.8 | loop fusion | flops 2752512 | bytes 5046272 | tf_op jit(solution)/shard_map/add | solution.py:15
  82.4 0.0 all-gather.2.cloned.1.call-update
  82.4 48.9 %all-gather.2.cloned.1.call-done = f32[2,32,14336]{2,0,1:T(2,128)} async-done(((f32[2,8,14336]{2,0,1:T(2,128)}), f32[2,32,14336]{2,0,1:T(2,128)}) %all-gather.2.cloned.1.call-update) | async-done | bytes 3670032 | tf_op jit(solution)/shard_map/all_gather | solution.py:50
  131.3 6.0 %copy.13 = f32[2,32,14336]{2,1,0:T(8,128)} copy(f32[2,32,14336]{2,0,1:T(2,128)} %all-gather.2.cloned.1.call-done) | data formatting | bytes 7340032 | tf_op jit(solution)/shard_map/all_gather | solution.py:50
  (2 shorter events, 0.0 us)
Async XLA Ops:
  6.5 11.1 %copy-start = (bf16[2,32,14336]{2,1,0:T(8,128)(2,1)S(1)}, bf16[2,32,14336]{2,1,0:T(8,128)(2,1)}, u32[]{:S(2)}) copy-start(bf16[2,32,14336]{2,1,0:T(8,128)(2,1)} %param.5) | copy-start | bytes 5505028
  12.4 28.0 %all-to-all-start = ((bf16[1,2,32,14336]{3,1,0,2:T(2,128)(2,1)}), bf16[1,2,32,14336]{3,1,0,2:T(2,128)(2,1)}, u32[]{:S(2)}, u32[]{:S(2)}) async-start(bf16[1,2,32,14336]{3,1,0,2:T(2,128)(2,1)} %copy.12), calls=%async_computation | async-start | bytes 3670016 | tf_op jit(solution)/shard_map/all_to_all | solution.py:38
  17.6 113.7 %all-gather.2.cloned.1.call-start = ((), (), s32[]{:S(2)}) async-start(), calls=%async_computation.1 | async-start | bytes 4587520 | tf_op jit(solution)/shard_map/all_gather | solution.py:50
Sparse Core Ops, SparseCore 0:
  82.5 48.7 all-gather.1
where the time goes:
time: 145 us; the launch traced here: 144 us
  waiting for transfers between devices  71.7 us (49%)
  other arithmetic  44.7 us (31%)
  between operations  13.4 us (9%)
  local copies, waits for them, and re-layouts  9.16 us (6%)
  starting transfers between devices  5.19 us (4%)
    all_gather x1, waiting for transfers between devices, on_device(): return lax.all_gather(merged_part, 'task', axis=1, tiled=True)  48.9 us
    all_to_all x1, waiting for transfers between devices, on_device(): lax.all_to_all(sendable, 'task', split_axis=2, concat_axis=0, tiled=True)  22.8 us
    convert_element_type x1, other arithmetic, statistics(): up_count = (trimmed > 0).astype(jnp.float32)  8.52 us
    max x1, other arithmetic, statistics(): upward = jnp.maximum(trimmed, 0.0)  8.46 us
    all_gather x1, local copies, waits for them, and re-layouts, on_device(): return lax.all_gather(merged_part, 'task', axis=1, tiled=True)  6 us
    reduce_sum x1, other arithmetic, on_device(): jnp.sum(upward, axis=0)  5.47 us
    reduce_sum x1, other arithmetic, on_device(): jnp.sum(down_count, axis=0)  5.29 us
    reduce_sum x1, other arithmetic, on_device(): jnp.sum(downward, axis=0)  5.25 us
  transfers between devices with their start and end apart: 2, of which 2 were waited for; matrix products, arithmetic and copies ran while one was open for 0% of the time, Pallas kernels for 0%

commit v1 on v0

v1 whole, which is shorter than its diff:
```python
import math

import jax
import jax.numpy as jnp
from jax import lax
from jax.sharding import PartitionSpec as P

BLOCK = 128
STEPS = 64
LEVELS = 255


def total(parts):
    out = parts[0]
    for part in parts[1:]:
        out = out + part
    return out


def elect(parts):
    wide = [part.astype(jnp.float32) for part in parts]
    upward = total([jnp.maximum(w, 0.0) for w in wide])
    downward = total([jnp.minimum(w, 0.0) for w in wide])
    up_count = total([(w > 0).astype(jnp.float32) for w in wide])
    down_count = total([(w < 0).astype(jnp.float32) for w in wide])
    balance = upward + downward
    side = jnp.where(balance > 0, upward, downward)
    count = jnp.where(balance > 0, up_count, down_count)
    return jnp.where(balance == 0, 0.0, side), jnp.maximum(count, 1.0)


def kept(keep_blocks, rows):
    row_start = lax.axis_index("dp") * rows
    if BLOCK % rows == 0:
        return lax.dynamic_slice_in_dim(keep_blocks, row_start // BLOCK, 1, 1)
    blocks = (row_start + jnp.arange(rows, dtype=jnp.int32)) // BLOCK
    return jnp.take(keep_blocks, blocks, axis=1)


def on_any_group(deltas, keep_blocks, base_weights):
    n = lax.axis_size("task")
    _, projections, rows, width = deltas.shape
    keep = kept(keep_blocks[0], rows)
    trimmed = jnp.where(keep[:, :, None] != 0, deltas[0], jnp.zeros((), deltas.dtype))
    split = trimmed.reshape(projections, n, rows // n, width).swapaxes(0, 1)
    arrived = lax.all_to_all(split, "task", split_axis=0, concat_axis=0, tiled=True)
    side, count = elect([arrived[i] for i in range(n)])
    agreed = lax.all_gather(side / count, "task", axis=1, tiled=True)
    return base_weights.astype(jnp.float32) + agreed


def on_square(deltas, keep_blocks, base_weights):
    n = 4
    me = lax.axis_index("task")
    _, projections, rows, width = deltas.shape
    share, half = rows // n, width // 2
    unit = STEPS * math.lcm(*range(1, n + 1))
    keep = kept(keep_blocks[0], rows)

    def permute(x, mask):
        return lax.ppermute(x, "task", [(i, i ^ mask) for i in range(n)])

    columns = []
    for p in range(projections):
        trimmed = jnp.where(keep[p][:, None] != 0, deltas[0, p], jnp.zeros((), deltas.dtype))
        pieces = trimmed.reshape(n, share, width)
        piece = [lax.dynamic_index_in_dim(pieces, me ^ m, 0, False) for m in range(n)]
        columns.append([piece[0]] + [permute(piece[m], m) for m in range(1, n)])
    outs = []
    for p in range(projections):
        side, count = elect(columns[p])
        code = jnp.round(side * (unit / count)).astype(jnp.int16)
        beside, above = permute(code, 1), permute(code, 2)
        across = jnp.concatenate(
            [permute(beside[:, :half], 2), permute(above[:, half:], 1)], 1
        )
        held = [code, beside, above, across]
        odd, high = (me & 1) == 1, (me & 2) == 2
        swapped = [jnp.where(odd, held[i ^ 1], held[i]) for i in range(n)]
        ordered = [jnp.where(high, swapped[i ^ 2], swapped[i]) for i in range(n)]
        agreed = jnp.concatenate(ordered, 0).astype(jnp.float32) * (1.0 / unit)
        outs.append(base_weights[p].astype(jnp.float32) + agreed)
    return jnp.stack(outs)


def on_device(deltas, keep_blocks, base_weights):
    n = lax.axis_size("task")
    codes = LEVELS * math.lcm(*range(1, n + 1))
    if n == 4 and deltas.shape[2] % n == 0 and codes < 2**15:
        return on_square(deltas, keep_blocks, base_weights)
    return on_any_group(deltas, keep_blocks, base_weights)


def solution(mesh):
    in_specs = (P("task", None, "dp", "mp"), P("task", None, None), P(None, "dp", "mp"))
    out_specs = P(None, "dp", "mp")
    return jax.shard_map(
        on_device, mesh=mesh, in_specs=in_specs, out_specs=out_specs, check_vma=False
    )
```

time: 145 us -> 51.4 us (0.35)
  waiting for transfers between devices: 71.7 us -> 18.6 us
  other arithmetic: 44.7 us -> 7.46 us
  starting transfers between devices: 5.19 us -> 19.7 us
  between operations: 13.4 us -> 1.4 us
  local copies, waits for them, and re-layouts: 9.16 us -> 4.02 us
    all_gather x1 -> x0, waiting for transfers between devices: 48.9 us -> none  [on_device(): return lax.all_gather(merged_part, 'task', axis=1, tiled=True)]
    all_to_all x1 -> x0, waiting for transfers between devices: 22.8 us -> none  [on_device(): lax.all_to_all(sendable, 'task', split_axis=2, concat_axis=0, tiled=True)]
    reduce_sum x4 -> x0, other arithmetic: 20.3 us -> none  [the longest x1 5.47 us: on_device(): jnp.sum(upward, axis=0)]
    ppermute x0 -> x14, starting transfers between devices: none -> 19.7 us  [permute(): return lax.ppermute(x, 'task', [(i, i ^ mask) for i in range(n)])]
    ppermute x0 -> x14, waiting for transfers between devices: none -> 18.6 us  [permute(): return lax.ppermute(x, 'task', [(i, i ^ mask) for i in range(n)])]
    convert_element_type x3 -> x2, other arithmetic: 11.2 us -> 2.54 us  [on_square(): code = jnp.round(side * (unit / count)).astype(jnp.int16)]
    max x1 -> x0, other arithmetic: 8.46 us -> none  [statistics(): upward = jnp.maximum(trimmed, 0.0)]
    all_gather x1 -> x0, local copies, waits for them, and re-layouts: 6 us -> none  [on_device(): return lax.all_gather(merged_part, 'task', axis=1, tiled=True)]
  transfers between devices with their start and end apart: 2 -> 14, of which waited for: 2 -> 8; matrix products, arithmetic and copies ran while one was open for 0% -> 7% of each run, Pallas kernels for 0% -> 0%
where the time goes in v1:
time: 51.4 us; the launch traced here: 51.2 us
  starting transfers between devices  19.7 us (38%)
  waiting for transfers between devices  18.6 us (36%)
  other arithmetic  7.46 us (15%)
  local copies, waits for them, and re-layouts  4.02 us (8%)
  between operations  1.4 us (3%)
    ppermute x14, starting transfers between devices, permute(): return lax.ppermute(x, 'task', [(i, i ^ mask) for i in range(n)])  19.7 us
    ppermute x14, waiting for transfers between devices, permute(): return lax.ppermute(x, 'task', [(i, i ^ mask) for i in range(n)])  18.6 us
    convert_element_type x2, other arithmetic, on_square(): code = jnp.round(side * (unit / count)).astype(jnp.int16)  2.54 us
    another operation x1, other arithmetic, on_square(): return jnp.stack(outs)  2.07 us
    select_n x1, other arithmetic, on_square(): jnp.where(keep[p][:, None] != 0, deltas[0, p], jnp.zeros((), deltas.dtype))  1.58 us
    squeeze x2, local copies, waits for them, and re-layouts, on_square(): lax.dynamic_index_in_dim(pieces, me ^ m, 0, False)  1.56 us
    slice x1, local copies, waits for them, and re-layouts, on_square(): keep[p][:, None] != 0  1.35 us
    unnamed x4, local copies, waits for them, and re-layouts  1.06 us
  transfers between devices with their start and end apart: 14, of which 8 were waited for; matrix products, arithmetic and copies ran while one was open for 7% of the time, Pallas kernels for 0%

profile of v1, /device:TPU:0, one launch (start us, length us, event | category | flops | bytes accessed | tf_op | source)
XLA Modules:
  0.0 51.2 jit_solution(8681094003236316898)
XLA Ops:
  0.0 1.3 %fusion.36 = (s32[1,1,1]{1,2,0:T(1,128)}, s32[1,1,1]{1,2,0:T(1,128)}) fusion(s32[1,2,1]{1,2,0:T(1,128)} %param.4), kind=kLoop, calls=%fused_computation.103 | loop fusion | bytes 16 | tf_op jit(solution)/shard_map/slice | solution.py:65
  2.6 1.6 %select_bitcast_fusion.1 = (bf16[4,8,14336]{2,1,0:T(8,128)(2,1)S(1)}, bf16[4,8,14336]{2,1,0:T(8,128)(2,1)S(1)}) fusion(bf16[1,2,32,14336]{3,2,1,0:T(8,128)(2,1)} %param.3, pred[]{:T(512)} %bitcast, pred[]{:T(512)} %bitcast.13), kind=kLoop, calls=%fused_computation.4 | loop fusion | flops 917504 | bytes 3670018 | tf_op jit(solution)/shard_map/jit(_where)/select_n | solution.py:65
  4.2 0.8 %dynamic-slice_bitcast_fusion.3 = (bf16[8,14336]{1,0:T(8,128)(2,1)}, bf16[8,14336]{1,0:T(8,128)(2,1)}, bf16[8,14336]{1,0:T(8,128)(2,1)S(1)}) fusion(bf16[4,8,14336]{2,1,0:T(8,128)(2,1)S(1)} %get-tuple-element.7, s32[]{:T(128)S(6)} %select_n.133, s32[]{:T(128)S(6)} %select_n.132, s32[]{:T(128)S(6)} %select_n.131), kind=kLoop, calls=%fused_computation.88 | loop fusion | bytes 1376268 | tf_op jit(solution)/shard_map/jit(dynamic_index_in_dim)/squeeze | solution.py:67
  5.0 3.9 %collective-permute-start.2 = (bf16[8,14336]{1,0:T(8,128)(2,1)}, bf16[8,14336]{1,0:T(8,128)(2,1)S(1)}, u32[]{:S(2)}, u32[]{:S(2)}) collective-permute-start(bf16[8,14336]{1,0:T(8,128)(2,1)} %get-tuple-element.13), channel_id=1, source_target_pairs={{0,6},{2,4},{4,2},{6,0},{1,7},{3,5},{5,3},{7,1},{8,14},{10,12},{12... | collective-permute-start | bytes 688136 | tf_op jit(solution)/shard_map/ppermute | solution.py:61
  9.0 0.5 collective-permute-start.1
  9.5 0.7 %dynamic-slice_bitcast_fusion = (bf16[8,14336]{1,0:T(8,128)(2,1)}, bf16[8,14336]{1,0:T(8,128)(2,1)S(1)}, bf16[8,14336]{1,0:T(8,128)(2,1)S(1)}) fusion(bf16[4,8,14336]{2,1,0:T(8,128)(2,1)S(1)} %get-tuple-element.8, s32[]{:T(128)S(6)} %select_n.133, s32[]{:T(128)S(6)} %select_n.132, s32[]{:T(128)S(6)} %select_n.131), kind=kLoop, calls=%fused_computation.81 | loop fusion | bytes 1376268 | tf_op jit(solution)/shard_map/jit(dynamic_index_in_dim)/squeeze | solution.py:67
  10.3 2.9 %collective-permute-start.9 = (bf16[8,14336]{1,0:T(8,128)(2,1)}, bf16[8,14336]{1,0:T(8,128)(2,1)S(1)}, u32[]{:S(2)}, u32[]{:S(2)}) collective-permute-start(bf16[8,14336]{1,0:T(8,128)(2,1)} %get-tuple-element.20), channel_id=1, source_target_pairs={{0,6},{2,4},{4,2},{6,0},{1,7},{3,5},{5,3},{7,1},{8,14},{10,12},{12... | collective-permute-start | bytes 688136 | tf_op jit(solution)/shard_map/ppermute | solution.py:61
  13.2 0.5 collective-permute-start.8
  13.7 2.0 %collective-permute-done.2 = bf16[8,14336]{1,0:T(8,128)(2,1)S(1)} collective-permute-done((bf16[8,14336]{1,0:T(8,128)(2,1)}, bf16[8,14336]{1,0:T(8,128)(2,1)S(1)}, u32[]{:S(2)}, u32[]{:S(2)}) %collective-permute-start.2) | collective-permute-done | bytes 229408 | tf_op jit(solution)/shard_map/ppermute | solution.py:61
  15.7 2.0 %collective-permute-start.7 = (bf16[8,14336]{1,0:T(8,128)(2,1)S(1)}, bf16[8,14336]{1,0:T(8,128)(2,1)S(1)}, u32[]{:S(2)}, u32[]{:S(2)}) collective-permute-start(bf16[8,14336]{1,0:T(8,128)(2,1)S(1)} %get-tuple-element.22), channel_id=1, source_target_pairs={{0,2},{2,0},{4,6},{6,4},{1,3},{3,1},{5,7},{7,5},{8,10},{10,8},{12,... | collective-permute-start | bytes 688136 | tf_op jit(solution)/shard_map/ppermute | solution.py:61
  17.6 3.0 %collective-permute-done.1 = bf16[8,14336]{1,0:T(8,128)(2,1)S(1)} collective-permute-done((bf16[8,14336]{1,0:T(8,128)(2,1)}, bf16[8,14336]{1,0:T(8,128)(2,1)S(1)}, u32[]{:S(2)}, u32[]{:S(2)}) %collective-permute-start.1) | collective-permute-done | bytes 229408 | tf_op jit(solution)/shard_map/ppermute | solution.py:61
  20.6 0.6 %collective-permute-done = bf16[8,14336]{1,0:T(8,128)(2,1)} collective-permute-done((bf16[8,14336]{1,0:T(8,128)(2,1)S(1)}, bf16[8,14336]{1,0:T(8,128)(2,1)}, u32[]{:S(2)}, u32[]{:S(2)}) %collective-permute-start) | collective-permute-done | bytes 229408 | tf_op jit(solution)/shard_map/ppermute | solution.py:61
  21.2 1.7 %fusion.34 = s16[8,14336]{1,0:T(8,128)(2,1)S(1)} fusion(bf16[8,14336]{1,0:T(8,128)(2,1)} %collective-permute-done, bf16[8,14336]{1,0:T(8,128)(2,1)S(1)} %collective-permute-done.1, bf16[8,14336]{1,0:T(8,128)(2,1)S(1)} %collective-permute-done.2, bf16[4,8,14336]{2,1,0:T(8,128)(2,1)S(1)} %get-tuple-element.7, s32[]{:T(128)S(6)} %select_n.130), kind=kLoop, calls=%fused_computation.75 | loop fusion | flops 5849088 | bytes 1146884 | tf_op jit(solution)/shard_map/convert_element_type | solution.py:72
  23.0 1.5 %collective-permute-start.5 = (s16[8,14336]{1,0:T(8,128)(2,1)S(1)}, s16[8,14336]{1,0:T(8,128)(2,1)S(1)}, u32[]{:S(2)}, u32[]{:S(2)}) collective-permute-start(s16[8,14336]{1,0:T(8,128)(2,1)S(1)} %fusion.34), channel_id=1, source_target_pairs={{0,4},{2,6},{4,0},{6,2},{1,5},{3,7},{5,1},{7,3},{8,12},{10,14},{12... | collective-permute-start | bytes 688136 | tf_op jit(solution)/shard_map/ppermute | solution.py:61
  24.4 1.5 %collective-permute-start.3 = (s16[8,14336]{1,0:T(8,128)(2,1)S(1)}, s16[8,14336]{1,0:T(8,128)(2,1)S(1)}, u32[]{:S(2)}, u32[]{:S(2)}) collective-permute-start(s16[8,14336]{1,0:T(8,128)(2,1)S(1)} %fusion.34), channel_id=1, source_target_pairs={{0,2},{2,0},{4,6},{6,4},{1,3},{3,1},{5,7},{7,5},{8,10},{10,8},{12,... | collective-permute-start | bytes 688136 | tf_op jit(solution)/shard_map/ppermute | solution.py:61
  25.9 3.7 %collective-permute-done.8 = bf16[8,14336]{1,0:T(8,128)(2,1)S(1)} collective-permute-done((bf16[8,14336]{1,0:T(8,128)(2,1)S(1)}, bf16[8,14336]{1,0:T(8,128)(2,1)S(1)}, u32[]{:S(2)}, u32[]{:S(2)}) %collective-permute-start.8) | collective-permute-done | bytes 229408 | tf_op jit(solution)/shard_map/ppermute | solution.py:61
  29.6 1.4 %collective-permute-done.7 = bf16[8,14336]{1,0:T(8,128)(2,1)S(1)} collective-permute-done((bf16[8,14336]{1,0:T(8,128)(2,1)S(1)}, bf16[8,14336]{1,0:T(8,128)(2,1)S(1)}, u32[]{:S(2)}, u32[]{:S(2)}) %collective-permute-start.7) | collective-permute-done | bytes 229408 | tf_op jit(solution)/shard_map/ppermute | solution.py:61
  31.0 0.8 %fusion.35 = s16[8,14336]{1,0:T(8,128)(2,1)S(1)} fusion(bf16[8,14336]{1,0:T(8,128)(2,1)S(1)} %collective-permute-done.7, bf16[8,14336]{1,0:T(8,128)(2,1)S(1)} %collective-permute-done.8, bf16[8,14336]{1,0:T(8,128)(2,1)S(1)} %collective-permute-done.9, bf16[4,8,14336]{2,1,0:T(8,128)(2,1)S(1)} %get-tuple-element.8, s32[]{:T(128)S(6)} %select_n.130), kind=kLoop, calls=%fused_computation.76 | loop fusion | flops 5849088 | bytes 1146884 | tf_op jit(solution)/shard_map/convert_element_type | solution.py:72
  31.8 0.4 collective-permute-start.12
  32.2 1.7 %collective-permute-start.10 = (s16[8,14336]{1,0:T(8,128)(2,1)S(1)}, s16[8,14336]{1,0:T(8,128)(2,1)S(1)}, u32[]{:S(2)}, u32[]{:S(2)}) collective-permute-start(s16[8,14336]{1,0:T(8,128)(2,1)S(1)} %fusion.35), channel_id=1, source_target_pairs={{0,2},{2,0},{4,6},{6,4},{1,3},{3,1},{5,7},{7,5},{8,10},{10,8},{12,... | collective-permute-start | bytes 688136 | tf_op jit(solution)/shard_map/ppermute | solution.py:61
  33.9 1.3 %collective-permute-done.3 = s16[8,14336]{1,0:T(8,128)(2,1)S(1)} collective-permute-done((s16[8,14336]{1,0:T(8,128)(2,1)S(1)}, s16[8,14336]{1,0:T(8,128)(2,1)S(1)}, u32[]{:S(2)}, u32[]{:S(2)}) %collective-permute-start.3) | collective-permute-done | bytes 229408 | tf_op jit(solution)/shard_map/ppermute | solution.py:61
  35.1 0.3 collective-permute-start.4
  35.5 2.1 %collective-permute-start.6 = (s16[8,7168]{1,0:T(8,128)(2,1)S(1)}, s16[8,7168]{1,0:T(8,128)(2,1)S(1)}, u32[]{:S(2)}, u32[]{:S(2)}) collective-permute-start(s16[8,7168]{1,0:T(8,128)(2,1)S(1)} %slice.43), channel_id=1, source_target_pairs={{0,2},{2,0},{4,6},{6,4},{1,3},{3,1},{5,7},{7,5},{8,10},{10,8},{12,... | collective-permute-start | bytes 344072 | tf_op jit(solution)/shard_map/ppermute | solution.py:61
  37.5 2.8 %collective-permute-done.12 = s16[8,14336]{1,0:T(8,128)(2,1)S(1)} collective-permute-done((s16[8,14336]{1,0:T(8,128)(2,1)S(1)}, s16[8,14336]{1,0:T(8,128)(2,1)S(1)}, u32[]{:S(2)}, u32[]{:S(2)}) %collective-permute-start.12) | collective-permute-done | bytes 229408 | tf_op jit(solution)/shard_map/ppermute | solution.py:61
  40.3 1.5 %collective-permute-start.13 = (s16[8,7168]{1,0:T(8,128)(2,1)S(1)}, s16[8,7168]{1,0:T(8,128)(2,1)S(1)}, u32[]{:S(2)}, u32[]{:S(2)}) collective-permute-start(s16[8,7168]{1,0:T(8,128)(2,1)S(1)} %slice.45), channel_id=1, source_target_pairs={{0,2},{2,0},{4,6},{6,4},{1,3},{3,1},{5,7},{7,5},{8,10},{10,8},{12,... | collective-permute-start | bytes 344072 | tf_op jit(solution)/shard_map/ppermute | solution.py:61
  41.9 0.9 %collective-permute-start.11 = (s16[8,7168]{1,0:T(8,128)(2,1)S(1)}, s16[8,7168]{1,0:T(8,128)(2,1)S(1)}, u32[]{:S(2)}, u32[]{:S(2)}) collective-permute-start(s16[8,7168]{1,0:T(8,128)(2,1)S(1)} %slice.44), channel_id=1, source_target_pairs={{0,4},{2,6},{4,0},{6,2},{1,5},{3,7},{5,1},{7,3},{8,12},{10,14},{12... | collective-permute-start | bytes 344072 | tf_op jit(solution)/shard_map/ppermute | solution.py:61
  42.8 3.9 %collective-permute-done.11 = s16[8,7168]{1,0:T(8,128)(2,1)S(1)} collective-permute-done((s16[8,7168]{1,0:T(8,128)(2,1)S(1)}, s16[8,7168]{1,0:T(8,128)(2,1)S(1)}, u32[]{:S(2)}, u32[]{:S(2)}) %collective-permute-start.11) | collective-permute-done | bytes 114720 | tf_op jit(solution)/shard_map/ppermute | solution.py:61
  46.8 0.2 select_bitcast_fusion.9
  47.0 0.2 select_bitcast_fusion.5
  47.3 1.0 %copy-done = bf16[2,32,14336]{2,1,0:T(8,128)(2,1)S(1)} copy-done((bf16[2,32,14336]{2,1,0:T(8,128)(2,1)S(1)}, bf16[2,32,14336]{2,1,0:T(8,128)(2,1)}, u32[]{:S(2)}) %copy-start) | copy-done | bytes 1835032
  48.3 0.8 %multiply_add_fusion.1 = (f32[1,32,14336]{2,1,0:T(8,128)S(1)}, f32[1,32,14336]{2,1,0:T(8,128)S(1)}) fusion(s16[1,8,14336]{2,1,0:T(8,128)(2,1)S(1)} %get-tuple-element.12, s16[1,8,14336]{2,1,0:T(8,128)(2,1)S(1)} %get-tuple-element.11, s16[1,8,14336]{2,1,0:T(8,128)(2,1)S(1)} %get-tuple-element.10, s16[1,8,14336]{2,1,0:T(8,128)(2,1)S(1)} %get-tuple-element.9, ...), kind=kLoop, calls=%fused_computation.2 | loop fusion | flops 6422528 | bytes 7340032 | tf_op jit(solution)/shard_map/add | solution.py:82
  49.1 2.1 %pad_maximum_fusion = f32[2,32,14336]{2,1,0:T(8,128)} fusion(f32[1,32,14336]{2,1,0:T(8,128)S(1)} %get-tuple-element.6, f32[1,32,14336]{2,1,0:T(8,128)S(1)} %get-tuple-element.5), kind=kLoop, calls=%fused_computation | loop fusion | flops 917504 | bytes 7340032 | tf_op jit(solution)/shard_map/stack | solution.py:83
  (16 shorter events, 0.2 us)
Async XLA Ops:
  5.0 10.6 %collective-permute-start.2 = (bf16[8,14336]{1,0:T(8,128)(2,1)}, bf16[8,14336]{1,0:T(8,128)(2,1)S(1)}, u32[]{:S(2)}, u32[]{:S(2)}) collective-permute-start(bf16[8,14336]{1,0:T(8,128)(2,1)} %get-tuple-element.13), channel_id=1, source_target_pairs={{0,6},{2,4},{4,2},{6,0},{1,7},{3,5},{5,3},{7,1},{8,14},{10,12},{12... | collective-permute-start | bytes 688136 | tf_op jit(solution)/shard_map/ppermute | solution.py:61
  9.0 11.7 %collective-permute-start.1 = (bf16[8,14336]{1,0:T(8,128)(2,1)}, bf16[8,14336]{1,0:T(8,128)(2,1)S(1)}, u32[]{:S(2)}, u32[]{:S(2)}) collective-permute-start(bf16[8,14336]{1,0:T(8,128)(2,1)} %get-tuple-element.14), channel_id=1, source_target_pairs={{0,4},{2,6},{4,0},{6,2},{1,5},{3,7},{5,1},{7,3},{8,12},{10,14},{12... | collective-permute-start | bytes 688136 | tf_op jit(solution)/shard_map/ppermute | solution.py:61
  9.5 11.8 %collective-permute-start = (bf16[8,14336]{1,0:T(8,128)(2,1)S(1)}, bf16[8,14336]{1,0:T(8,128)(2,1)}, u32[]{:S(2)}, u32[]{:S(2)}) collective-permute-start(bf16[8,14336]{1,0:T(8,128)(2,1)S(1)} %get-tuple-element.15), channel_id=1, source_target_pairs={{0,2},{2,0},{4,6},{6,4},{1,3},{3,1},{5,7},{7,5},{8,10},{10,8},{12,... | collective-permute-start | bytes 688136 | tf_op jit(solution)/shard_map/ppermute | solution.py:61
  10.3 15.6 %collective-permute-start.9 = (bf16[8,14336]{1,0:T(8,128)(2,1)}, bf16[8,14336]{1,0:T(8,128)(2,1)S(1)}, u32[]{:S(2)}, u32[]{:S(2)}) collective-permute-start(bf16[8,14336]{1,0:T(8,128)(2,1)} %get-tuple-element.20), channel_id=1, source_target_pairs={{0,6},{2,4},{4,2},{6,0},{1,7},{3,5},{5,3},{7,1},{8,14},{10,12},{12... | collective-permute-start | bytes 688136 | tf_op jit(solution)/shard_map/ppermute | solution.py:61
  13.2 16.4 %collective-permute-start.8 = (bf16[8,14336]{1,0:T(8,128)(2,1)S(1)}, bf16[8,14336]{1,0:T(8,128)(2,1)S(1)}, u32[]{:S(2)}, u32[]{:S(2)}) collective-permute-start(bf16[8,14336]{1,0:T(8,128)(2,1)S(1)} %get-tuple-element.21), channel_id=1, source_target_pairs={{0,4},{2,6},{4,0},{6,2},{1,5},{3,7},{5,1},{7,3},{8,12},{10,14},{12... | collective-permute-start | bytes 688136 | tf_op jit(solution)/shard_map/ppermute | solution.py:61
  15.7 15.3 %collective-permute-start.7 = (bf16[8,14336]{1,0:T(8,128)(2,1)S(1)}, bf16[8,14336]{1,0:T(8,128)(2,1)S(1)}, u32[]{:S(2)}, u32[]{:S(2)}) collective-permute-start(bf16[8,14336]{1,0:T(8,128)(2,1)S(1)} %get-tuple-element.22), channel_id=1, source_target_pairs={{0,2},{2,0},{4,6},{6,4},{1,3},{3,1},{5,7},{7,5},{8,10},{10,8},{12,... | collective-permute-start | bytes 688136 | tf_op jit(solution)/shard_map/ppermute | solution.py:61
  23.0 12.5 %collective-permute-start.5 = (s16[8,14336]{1,0:T(8,128)(2,1)S(1)}, s16[8,14336]{1,0:T(8,128)(2,1)S(1)}, u32[]{:S(2)}, u32[]{:S(2)}) collective-permute-start(s16[8,14336]{1,0:T(8,128)(2,1)S(1)} %fusion.34), channel_id=1, source_target_pairs={{0,4},{2,6},{4,0},{6,2},{1,5},{3,7},{5,1},{7,3},{8,12},{10,14},{12... | collective-permute-start | bytes 688136 | tf_op jit(solution)/shard_map/ppermute | solution.py:61
  24.4 10.7 %collective-permute-start.3 = (s16[8,14336]{1,0:T(8,128)(2,1)S(1)}, s16[8,14336]{1,0:T(8,128)(2,1)S(1)}, u32[]{:S(2)}, u32[]{:S(2)}) collective-permute-start(s16[8,14336]{1,0:T(8,128)(2,1)S(1)} %fusion.34), channel_id=1, source_target_pairs={{0,2},{2,0},{4,6},{6,4},{1,3},{3,1},{5,7},{7,5},{8,10},{10,8},{12,... | collective-permute-start | bytes 688136 | tf_op jit(solution)/shard_map/ppermute | solution.py:61
  31.8 8.5 %collective-permute-start.12 = (s16[8,14336]{1,0:T(8,128)(2,1)S(1)}, s16[8,14336]{1,0:T(8,128)(2,1)S(1)}, u32[]{:S(2)}, u32[]{:S(2)}) collective-permute-start(s16[8,14336]{1,0:T(8,128)(2,1)S(1)} %fusion.35), channel_id=1, source_target_pairs={{0,4},{2,6},{4,0},{6,2},{1,5},{3,7},{5,1},{7,3},{8,12},{10,14},{12... | collective-permute-start | bytes 688136 | tf_op jit(solution)/shard_map/ppermute | solution.py:61
  32.2 9.7 %collective-permute-start.10 = (s16[8,14336]{1,0:T(8,128)(2,1)S(1)}, s16[8,14336]{1,0:T(8,128)(2,1)S(1)}, u32[]{:S(2)}, u32[]{:S(2)}) collective-permute-start(s16[8,14336]{1,0:T(8,128)(2,1)S(1)} %fusion.35), channel_id=1, source_target_pairs={{0,2},{2,0},{4,6},{6,4},{1,3},{3,1},{5,7},{7,5},{8,10},{10,8},{12,... | collective-permute-start | bytes 688136 | tf_op jit(solution)/shard_map/ppermute | solution.py:61
  35.1 7.7 %collective-permute-start.4 = (s16[8,7168]{1,0:T(8,128)(2,1)S(1)}, s16[8,7168]{1,0:T(8,128)(2,1)S(1)}, u32[]{:S(2)}, u32[]{:S(2)}) collective-permute-start(s16[8,7168]{1,0:T(8,128)(2,1)S(1)} %slice.42), channel_id=1, source_target_pairs={{0,4},{2,6},{4,0},{6,2},{1,5},{3,7},{5,1},{7,3},{8,12},{10,14},{12... | collective-permute-start | bytes 344072 | tf_op jit(solution)/shard_map/ppermute | solution.py:61
  35.5 11.3 %collective-permute-start.6 = (s16[8,7168]{1,0:T(8,128)(2,1)S(1)}, s16[8,7168]{1,0:T(8,128)(2,1)S(1)}, u32[]{:S(2)}, u32[]{:S(2)}) collective-permute-start(s16[8,7168]{1,0:T(8,128)(2,1)S(1)} %slice.43), channel_id=1, source_target_pairs={{0,2},{2,0},{4,6},{6,4},{1,3},{3,1},{5,7},{7,5},{8,10},{10,8},{12,... | collective-permute-start | bytes 344072 | tf_op jit(solution)/shard_map/ppermute | solution.py:61
  40.3 6.4 %collective-permute-start.13 = (s16[8,7168]{1,0:T(8,128)(2,1)S(1)}, s16[8,7168]{1,0:T(8,128)(2,1)S(1)}, u32[]{:S(2)}, u32[]{:S(2)}) collective-permute-start(s16[8,7168]{1,0:T(8,128)(2,1)S(1)} %slice.45), channel_id=1, source_target_pairs={{0,2},{2,0},{4,6},{6,4},{1,3},{3,1},{5,7},{7,5},{8,10},{10,8},{12,... | collective-permute-start | bytes 344072 | tf_op jit(solution)/shard_map/ppermute | solution.py:61
  41.9 4.9 %collective-permute-start.11 = (s16[8,7168]{1,0:T(8,128)(2,1)S(1)}, s16[8,7168]{1,0:T(8,128)(2,1)S(1)}, u32[]{:S(2)}, u32[]{:S(2)}) collective-permute-start(s16[8,7168]{1,0:T(8,128)(2,1)S(1)} %slice.44), channel_id=1, source_target_pairs={{0,4},{2,6},{4,0},{6,2},{1,5},{3,7},{5,1},{7,3},{8,12},{10,14},{12... | collective-permute-start | bytes 344072 | tf_op jit(solution)/shard_map/ppermute | solution.py:61
  46.8 1.5 %copy-start = (bf16[2,32,14336]{2,1,0:T(8,128)(2,1)S(1)}, bf16[2,32,14336]{2,1,0:T(8,128)(2,1)}, u32[]{:S(2)}) copy-start(bf16[2,32,14336]{2,1,0:T(8,128)(2,1)} %param.5) | copy-start | bytes 5505028
